TPU v7x, 32 devices: a whole 2x2x4 slice. The times are simulated.
32 devices in a mesh: dp: 8 (over y, x, core), mp: 4 (over z).
Axes of the slice: x: 2, y: 2, z: 4, core: 2. Of those that a mesh axis runs over, the one named last changes fastest.
Arguments:
- tokens: bfloat16 [512, 8192], P('mp', 'dp'), may hold values from -6 to 6
- cotangent: bfloat16 [512, 8192], P('mp', 'dp'), may hold values from -1.5 to 1.5
- gate_weight: bfloat16 [8192, 14336], P('dp', 'mp'), may hold values from -0.0625 to 0.0625
- up_weight: bfloat16 [8192, 14336], P('dp', 'mp'), may hold values from -0.0625 to 0.0625
- down_weight: bfloat16 [14336, 8192], P('mp', 'dp'), may hold values from -0.046875 to 0.046875
Outputs:
- output: bfloat16 [512, 8192], P('mp', 'dp')
- grad_input: bfloat16 [512, 8192], P('mp', 'dp')
- grad_gate: bfloat16 [8192, 14336], P('dp', 'mp')
- grad_up: bfloat16 [8192, 14336], P('dp', 'mp')
- grad_down: bfloat16 [14336, 8192], P('mp', 'dp')
All inputs are finite; a program needn't handle non-finite values.
Results may differ from a plain program's by a relative error of at most 0.013.
Values may be sent and summed in bfloat16 or wider, within the bound.
No kernel may reach another device: no remote copies, remote signals or barrier semaphores. Data moves between devices by JAX's collectives and lax.ppermute only.
A program may use at most 128 MiB of HBM per device.

v0:
```python
import jax
import jax.numpy as jnp
from jax import lax
from jax.sharding import PartitionSpec as P


def contract(left, right, left_dim, right_dim):
    return lax.dot_general(
        left, right, (((left_dim,), (right_dim,)), ((), ())), preferred_element_type=jnp.float32
    )


def per_device(tokens, cotangent, gate_weight, up_weight, down_weight):
    all_tokens, all_cotangent = (
        lax.all_gather(tokens, "mp", axis=0, tiled=True),
        lax.all_gather(cotangent, "mp", axis=0, tiled=True),
    )
    columns = gate_weight.shape[1]
    rows = all_tokens
    stacked = lax.psum_scatter(
        jnp.concatenate(
            [
                jnp.dot(rows, gate_weight, preferred_element_type=jnp.float32),
                jnp.dot(rows, up_weight, preferred_element_type=jnp.float32),
            ],
            axis=1,
        ),
        "dp",
        scatter_dimension=0,
        tiled=True,
    )
    gate = stacked[:, :columns]
    up = stacked[:, columns:]
    sig = jax.nn.sigmoid(gate)
    hidden = (gate * sig * up).astype(jnp.bfloat16)
    all_hidden = lax.all_gather(hidden, "dp", axis=0, tiled=True)
    rows = all_hidden
    output = lax.psum_scatter(
        jnp.dot(rows, down_weight, preferred_element_type=jnp.float32).astype(jnp.bfloat16),
        "mp",
        scatter_dimension=0,
        tiled=True,
    )
    grad_down = contract(all_hidden, all_cotangent, 0, 0).astype(jnp.bfloat16)
    rows = all_cotangent
    d_hidden = lax.psum_scatter(
        contract(rows, down_weight, 1, 1), "dp", scatter_dimension=0, tiled=True
    )
    d_gate = (d_hidden * up * sig * (1.0 + gate * (1.0 - sig))).astype(jnp.bfloat16)
    d_up = (d_hidden * gate * sig).astype(jnp.bfloat16)
    all_d_gate, all_d_up = (
        lax.all_gather(d_gate, "dp", axis=0, tiled=True),
        lax.all_gather(d_up, "dp", axis=0, tiled=True),
    )
    grad_gate = contract(all_tokens, all_d_gate, 0, 0).astype(jnp.bfloat16)
    grad_up = contract(all_tokens, all_d_up, 0, 0).astype(jnp.bfloat16)
    grad_input = lax.psum_scatter(
        (contract(all_d_gate, gate_weight, 1, 1) + contract(all_d_up, up_weight, 1, 1)).astype(
            jnp.bfloat16
        ),
        "mp",
        scatter_dimension=0,
        tiled=True,
    )
    return (output, grad_input, grad_gate, grad_up, grad_down)


def solution(mesh):
    placed = (P("mp", "dp"), P("mp", "dp"), P("dp", "mp"), P("dp", "mp"), P("mp", "dp"))
    return jax.shard_map(
        per_device,
        mesh=mesh,
        in_specs=placed,
        out_specs=(P("mp", "dp"), P("mp", "dp"), P("dp", "mp"), P("dp", "mp"), P("mp", "dp")),
        check_vma=False,
    )
```

profile of v0, /device:TPU:0, one launch (start us, length us, event | category | flops | bytes accessed | tf_op | source)
XLA Modules:
  0.0 424.4 jit_solution(3029264662274093701)
XLA Ops:
  7.2 0.7 all-gather.10.cloned.1.call-update
  7.9 0.7 all-gather.6.cloned.1.call-update
  8.7 31.6 %all-gather.10.cloned.1.call-done = bf16[512,1024]{1,0:T(8,128)(2,1)} async-done(((bf16[128,1024]{1,0:T(8,128)(2,1)}), bf16[512,1024]{1,0:T(8,128)(2,1)}) %all-gather.10.cloned.1.call-update) | async-done | bytes 1048592 | tf_op jit(solution)/shard_map/all_gather | solution.py:16
  40.3 10.5 %fusion.4 = f32[512,3584]{1,0:T(8,128)} fusion(bf16[512,1024]{1,0:T(8,128)(2,1)} %all-gather.10.cloned.1.call-done, bf16[3584,1024]{1,0:T(8,128)(2,1)} %param.9), kind=kOutput, calls=%fused_computation.14 | convolution fusion | flops 3758096384 | bytes 15728640 | tf_op jit(solution)/shard_map/dot_general | solution.py:8
  50.8 18.4 %all-gather.6.cloned.1.call-done = bf16[512,1024]{1,0:T(8,128)(2,1)} async-done(((bf16[128,1024]{1,0:T(8,128)(2,1)}), bf16[512,1024]{1,0:T(8,128)(2,1)}) %all-gather.6.cloned.1.call-update) | async-done | bytes 1048592 | tf_op jit(solution)/shard_map/all_gather | solution.py:15
  69.2 7.4 %fusion.2 = f32[512,3584]{1,0:T(8,128)S(1)} fusion(bf16[512,1024]{1,0:T(8,128)(2,1)} %all-gather.6.cloned.1.call-done, bf16[1024,3584]{1,0:T(8,128)(2,1)} %param.7), kind=kOutput, calls=%fused_computation.12 | convolution fusion | flops 3758096384 | bytes 15728640 | tf_op jit(solution)/shard_map/dot_general | solution.py:23
  76.7 6.8 %fusion.3 = f32[512,3584]{1,0:T(8,128)S(1)} fusion(bf16[512,1024]{1,0:T(8,128)(2,1)S(1)} %copy-done.1, bf16[1024,3584]{1,0:T(8,128)(2,1)} %param.8), kind=kOutput, calls=%fused_computation.13 | convolution fusion | flops 3758096384 | bytes 15728640 | tf_op jit(solution)/shard_map/dot_general | solution.py:24
  83.5 6.4 %pad_maximum_fusion = f32[512,7168]{1,0:T(8,128)} fusion(f32[512,3584]{1,0:T(8,128)S(1)} %fusion.3, f32[512,3584]{1,0:T(8,128)S(1)} %fusion.2), kind=kLoop, calls=%fused_computation | loop fusion | flops 3670016 | bytes 29360128 | tf_op jit(solution)/shard_map/concatenate | solution.py:21
  90.0 49.6 %reduce-scatter.9.cloned.1.call-done = f32[64,3584]{1,0:T(8,128)} async-done(((f32[512,3584]{1,0:T(8,128)}), f32[64,3584]{1,0:T(8,128)}) %reduce-scatter.9.cloned.1.call-update) | async-done | bytes 917520 | tf_op jit(solution)/shard_map/reduce_scatter | solution.py:46
  139.6 108.0 %reduce-scatter.5.cloned.1.call-done = f32[64,7168]{1,0:T(8,128)} async-done(((f32[512,7168]{1,0:T(8,128)}), f32[64,7168]{1,0:T(8,128)}) %reduce-scatter.5.cloned.1.call-update) | async-done | bytes 1835024 | tf_op jit(solution)/shard_map/reduce_scatter | solution.py:20
  247.6 3.2 multiply_convert_fusion
  251.5 0.7 all-gather.8.cloned.1.call-update
  252.2 33.2 %all-gather.12.cloned.1.call-done = bf16[512,3584]{1,0:T(8,128)(2,1)} async-done(((bf16[64,3584]{1,0:T(8,128)(2,1)}), bf16[512,3584]{1,0:T(8,128)(2,1)}) %all-gather.12.cloned.1.call-update) | async-done | bytes 3670032 | tf_op jit(solution)/shard_map/all_gather | solution.py:52
  285.4 7.4 %fusion.5 = f32[512,1024]{1,0:T(8,128)S(1)} fusion(bf16[512,3584]{1,0:T(8,128)(2,1)} %all-gather.12.cloned.1.call-done, bf16[1024,3584]{1,0:T(8,128)(2,1)} %param.7), kind=kOutput, calls=%fused_computation.15 | convolution fusion | flops 3758096384 | bytes 13107200 | tf_op jit(solution)/shard_map/dot_general | solution.py:8
  292.7 29.4 %all-gather.14.cloned.1.call-done = bf16[512,3584]{1,0:T(8,128)(2,1)} async-done(((bf16[64,3584]{1,0:T(8,128)(2,1)}), bf16[512,3584]{1,0:T(8,128)(2,1)}) %all-gather.14.cloned.1.call-update) | async-done | bytes 3670032 | tf_op jit(solution)/shard_map/all_gather | solution.py:53
  322.1 9.2 %add_convert_fusion = bf16[512,1024]{1,0:T(8,128)(2,1)} fusion(f32[512,1024]{1,0:T(8,128)S(1)} %fusion.5, bf16[512,3584]{1,0:T(8,128)(2,1)} %all-gather.14.cloned.1.call-done, bf16[1024,3584]{1,0:T(8,128)(2,1)} %param.8), kind=kOutput, calls=%fused_computation.6 | convolution fusion | flops 3759144960 | bytes 14155776 | tf_op jit(solution)/shard_map/dot_general | solution.py:8
  331.6 27.4 %all-gather.8.cloned.1.call-done = bf16[512,3584]{1,0:T(8,128)(2,1)} async-done(((bf16[64,3584]{1,0:T(8,128)(2,1)}), bf16[512,3584]{1,0:T(8,128)(2,1)}) %all-gather.8.cloned.1.call-update) | async-done | bytes 3670032 | tf_op jit(solution)/shard_map/all_gather | solution.py:36
  359.0 9.1 %convolution_convert_fusion.3 = bf16[512,1024]{1,0:T(8,128)(2,1)} fusion(bf16[512,3584]{1,0:T(8,128)(2,1)} %all-gather.8.cloned.1.call-done, bf16[3584,1024]{1,0:T(8,128)(2,1)} %param.9), kind=kOutput, calls=%fused_computation.7 | convolution fusion | flops 3758620672 | bytes 12058624 | tf_op jit(solution)/shard_map/dot_general | solution.py:39
  368.1 8.1 %fusion = bf16[1024,3584]{0,1:T(8,128)(2,1)} fusion(bf16[512,3584]{1,0:T(8,128)(2,1)} %all-gather.12.cloned.1.call-done, bf16[512,1024]{1,0:T(8,128)(2,1)S(1)} %copy-done.1), kind=kOutput, calls=%fused_computation.4 | convolution fusion | flops 3761766400 | bytes 12058624 | tf_op jit(solution)/shard_map/dot_general | solution.py:8
  376.2 10.0 %copy.10 = bf16[1024,3584]{1,0:T(8,128)(2,1)} copy(bf16[1024,3584]{0,1:T(8,128)(2,1)} %fusion) | data formatting | bytes 14680064
  386.2 8.1 %fusion.1 = bf16[1024,3584]{0,1:T(8,128)(2,1)} fusion(bf16[512,3584]{1,0:T(8,128)(2,1)} %all-gather.14.cloned.1.call-done, bf16[512,1024]{1,0:T(8,128)(2,1)S(1)} %copy-done.1), kind=kOutput, calls=%fused_computation.5 | convolution fusion | flops 3761766400 | bytes 12058624 | tf_op jit(solution)/shard_map/dot_general | solution.py:8
  394.3 10.0 %copy.11 = bf16[1024,3584]{1,0:T(8,128)(2,1)} copy(bf16[1024,3584]{0,1:T(8,128)(2,1)} %fusion.1) | data formatting | bytes 14680064
  404.4 8.1 %convolution_convert_fusion = bf16[3584,1024]{1,0:T(8,128)(2,1)} fusion(bf16[512,3584]{1,0:T(8,128)(2,1)} %all-gather.8.cloned.1.call-done, bf16[512,1024]{1,0:T(8,128)(2,1)S(1)} %copy-done), kind=kOutput, calls=%fused_computation.1 | convolution fusion | flops 3761766400 | bytes 12058624 | tf_op jit(solution)/shard_map/dot_general | solution.py:8
  412.5 5.4 %reduce-scatter.7.cloned.1.call-done = bf16[128,1024]{1,0:T(8,128)(2,1)} async-done(((bf16[512,1024]{1,0:T(8,128)(2,1)}), bf16[128,1024]{1,0:T(8,128)(2,1)}) %reduce-scatter.7.cloned.1.call-update) | async-done | bytes 262160 | tf_op jit(solution)/shard_map/reduce_scatter | solution.py:38
  (20 shorter events, 1.2 us)
Async XLA Ops:
  7.2 33.1 %all-gather.10.cloned.1.call-start = ((), (), s32[]{:S(2)}) async-start(), calls=%async_computation.8 | async-start | bytes 1310720 | tf_op jit(solution)/shard_map/all_gather | solution.py:16
  7.9 61.3 %all-gather.6.cloned.1.call-start = ((), (), s32[]{:S(2)}) async-start(), calls=%async_computation.4 | async-start | bytes 1310720 | tf_op jit(solution)/shard_map/all_gather | solution.py:15
  8.6 130.9 %reduce-scatter.9.cloned.1.call-start = ((), (), s32[]{:S(2)}) async-start(), calls=%async_computation.9 | async-start | bytes 8257536 | tf_op jit(solution)/shard_map/reduce_scatter | solution.py:46
  50.8 196.8 %reduce-scatter.5.cloned.1.call-start = ((), (), s32[]{:S(2)}) async-start(), calls=%async_computation.5 | async-start | bytes 16515072 | tf_op jit(solution)/shard_map/reduce_scatter | solution.py:20
  69.2 7.5 %copy-start.1 = (bf16[512,1024]{1,0:T(8,128)(2,1)S(1)}, bf16[512,1024]{1,0:T(8,128)(2,1)}, u32[]{:S(2)}) copy-start(bf16[512,1024]{1,0:T(8,128)(2,1)} %all-gather.6.cloned.1.call-done) | copy-start | bytes 3145732
  89.9 195.5 %all-gather.12.cloned.1.call-start = ((), (), s32[]{:S(2)}) async-start(), calls=%async_computation.10 | async-start | bytes 4128768 | tf_op jit(solution)/shard_map/all_gather | solution.py:52
  250.8 71.3 %all-gather.14.cloned.1.call-start = ((), (), s32[]{:S(2)}) async-start(), calls=%async_computation.11 | async-start | bytes 4128768 | tf_op jit(solution)/shard_map/all_gather | solution.py:53
  251.4 107.6 %all-gather.8.cloned.1.call-start = ((), (), s32[]{:S(2)}) async-start(), calls=%async_computation.6 | async-start | bytes 4128768 | tf_op jit(solution)/shard_map/all_gather | solution.py:36
  252.2 160.3 %reduce-scatter.11.cloned.1.call-start = ((), (), s32[]{:S(2)}) async-start(), calls=%async_computation.12 | async-start | bytes 1310720 | tf_op jit(solution)/shard_map/reduce_scatter | solution.py:57
  331.3 86.5 %reduce-scatter.7.cloned.1.call-start = ((), (), s32[]{:S(2)}) async-start(), calls=%async_computation.7 | async-start | bytes 1310720 | tf_op jit(solution)/shard_map/reduce_scatter | solution.py:38
  394.3 10.1 %copy-start = (bf16[512,1024]{1,0:T(8,128)(2,1)S(1)}, bf16[512,1024]{1,0:T(8,128)(2,1)}, u32[]{:S(2)}) copy-start(bf16[512,1024]{1,0:T(8,128)(2,1)} %all-gather.10.cloned.1.call-done) | copy-start | bytes 3145732
Sparse Core Ops, SparseCore 0:
  9.5 30.6 all-gather.9
  41.8 27.3 all-gather.5
  73.2 66.3 reduce-scatter.8
  142.9 104.5 reduce-scatter.4
  250.9 34.3 all-gather.11
  287.7 34.3 all-gather.13
  324.6 34.3 all-gather.7
  361.8 27.2 reduce-scatter.10
  392.0 25.7 reduce-scatter.6
where the time goes:
time: 425 us; the launch traced here: 424 us
  waiting for transfers between devices  306 us (72%)
  matrix products  74.8 us (18%)
  local copies, waits for them, and re-layouts  20 us (5%)
  between operations  13.9 us (3%)
  other arithmetic  9.61 us (2%)
    reduce_scatter x1, waiting for transfers between devices, per_device(): lax.psum_scatter(jnp.concatenate([jnp.dot(rows, gate_weight, preferred_el...  108 us
    dot_general x6, matrix products, contract(): lax.dot_general(left, right, (((left_dim,), (right_dim,)), ((), ())), pre...  51.4 us
    reduce_scatter x1, waiting for transfers between devices, per_device(): lax.psum_scatter(contract(rows, down_weight, 1, 1), 'dp', scatter_dimensi...  49.6 us
    all_gather x1, waiting for transfers between devices, per_device(): lax.all_gather(d_gate, 'dp', axis=0, tiled=True)  33.2 us
    all_gather x1, waiting for transfers between devices, per_device(): lax.all_gather(cotangent, 'mp', axis=0, tiled=True)  31.6 us
    all_gather x1, waiting for transfers between devices, per_device(): lax.all_gather(d_up, 'dp', axis=0, tiled=True)  29.4 us
    all_gather x1, waiting for transfers between devices, per_device(): all_hidden = lax.all_gather(hidden, 'dp', axis=0, tiled=True)  27.4 us
    unnamed x6, local copies, waits for them, and re-layouts  20 us
  transfers between devices with their start and end apart: 9, of which 8 were waited for; matrix products, arithmetic and copies ran while one was open for 24% of the time, Pallas kernels for 0%

commit v1 on v0

--- a/solution.py
+++ b/solution.py
@@ -33,7 +33,12 @@
     up = stacked[:, columns:]
     sig = jax.nn.sigmoid(gate)
     hidden = (gate * sig * up).astype(jnp.bfloat16)
-    all_hidden = lax.all_gather(hidden, "dp", axis=0, tiled=True)
+    ring = [hidden]
+    for hop in range(7):
+        ring.append(lax.ppermute(ring[-1], "dp", [(dev, (dev + 1) % 8) for dev in range(8)]))
+    all_hidden = jnp.roll(
+        jnp.concatenate(ring[::-1], axis=0), (lax.axis_index("dp") + 1) * ring[0].shape[0], axis=0
+    )
     rows = all_hidden
     output = lax.psum_scatter(
         jnp.dot(rows, down_weight, preferred_element_type=jnp.float32).astype(jnp.bfloat16),

time: 425 us -> 416 us (0.979)
  waiting for transfers between devices: 306 us -> 295 us
  local copies, waits for them, and re-layouts: 20 us -> 25.5 us
    ppermute x0 -> x7, waiting for transfers between devices: none -> 72.2 us  [per_device(): lax.ppermute(ring[-1], 'dp', [(dev, (dev + 1) % 8) for dev in range(8)])]
    all_gather x1, waiting for transfers between devices: 33.2 us -> 0.02 us  [per_device(): lax.all_gather(d_gate, 'dp', axis=0, tiled=True)]
    all_gather x1 -> x0, waiting for transfers between devices: 27.4 us -> none  [per_device(): all_hidden = lax.all_gather(hidden, 'dp', axis=0, tiled=True)]
    all_gather x1, waiting for transfers between devices: 29.4 us -> 6.12 us  [per_device(): lax.all_gather(d_up, 'dp', axis=0, tiled=True)]
    reduce_scatter x1, waiting for transfers between devices: 0.01 us -> 7.13 us  [per_device(): lax.psum_scatter((contract(all_d_gate, gate_weight, 1, 1) + contract(all_...]
    unnamed x6 -> x27, local copies, waits for them, and re-layouts: 20 us -> 25.5 us
    reduce_scatter x1, waiting for transfers between devices: 5.36 us -> 0.01 us  [per_device(): lax.psum_scatter(jnp.dot(rows, down_weight, preferred_element_type=jnp.fl...]
  transfers between devices with their start and end apart: 9 -> 15, of which waited for: 8 -> 13; matrix products, arithmetic and copies ran while one was open for 24% -> 24% of each run, Pallas kernels for 0% -> 0%
where the time goes in v1:
time: 416 us
  waiting for transfers between devices  295 us (71%)
  matrix products  71.2 us (17%)
  local copies, waits for them, and re-layouts  25.5 us (6%)
  between operations  14.4 us (3%)
  other arithmetic  9.5 us (2%)
    reduce_scatter x1, waiting for transfers between devices, per_device(): lax.psum_scatter(jnp.concatenate([jnp.dot(rows, gate_weight, preferred_el...  108 us
    ppermute x7, waiting for transfers between devices, per_device(): lax.ppermute(ring[-1], 'dp', [(dev, (dev + 1) % 8) for dev in range(8)])  72.2 us
    reduce_scatter x1, waiting for transfers between devices, per_device(): lax.psum_scatter(contract(rows, down_weight, 1, 1), 'dp', scatter_dimensi...  49.6 us
    dot_general x6, matrix products, contract(): lax.dot_general(left, right, (((left_dim,), (right_dim,)), ((), ())), pre...  49.6 us
    all_gather x1, waiting for transfers between devices, per_device(): lax.all_gather(cotangent, 'mp', axis=0, tiled=True)  31.6 us
    unnamed x27, local copies, waits for them, and re-layouts  25.5 us
    all_gather x1, waiting for transfers between devices, per_device(): lax.all_gather(tokens, 'mp', axis=0, tiled=True)  18.4 us
  transfers between devices with their start and end apart: 15, of which 13 were waited for; matrix products, arithmetic and copies ran while one was open for 24% of the time, Pallas kernels for 0%

profile of v1, /device:TPU:0, one launch (start us, length us, event | category | flops | bytes accessed | tf_op | source)
XLA Modules:
  0.0 415.7 jit_solution(14284246303761192209)
XLA Ops:
  8.7 31.6 %all-gather.7.cloned.1.call-done = bf16[512,1024]{1,0:T(8,128)(2,1)} async-done(((bf16[128,1024]{1,0:T(8,128)(2,1)}), bf16[512,1024]{1,0:T(8,128)(2,1)}) %all-gather.7.cloned.1.call-update) | async-done | bytes 1048592 | tf_op jit(solution)/shard_map/all_gather | solution.py:16
  40.3 10.5 %fusion.12 = f32[512,3584]{1,0:T(8,128)} fusion(bf16[512,1024]{1,0:T(8,128)(2,1)} %all-gather.7.cloned.1.call-done, bf16[3584,1024]{1,0:T(8,128)(2,1)} %param.9), kind=kOutput, calls=%fused_computation.35 | convolution fusion | flops 3758096384 | bytes 15728640 | tf_op jit(solution)/shard_map/dot_general | solution.py:8
  50.8 18.4 %all-gather.5.cloned.1.call-done = bf16[512,1024]{1,0:T(8,128)(2,1)} async-done(((bf16[128,1024]{1,0:T(8,128)(2,1)}), bf16[512,1024]{1,0:T(8,128)(2,1)}) %all-gather.5.cloned.1.call-update) | async-done | bytes 1048592 | tf_op jit(solution)/shard_map/all_gather | solution.py:15
  69.2 7.4 %fusion.10 = f32[512,3584]{1,0:T(8,128)S(1)} fusion(bf16[512,1024]{1,0:T(8,128)(2,1)} %all-gather.5.cloned.1.call-done, bf16[1024,3584]{1,0:T(8,128)(2,1)} %param.7), kind=kOutput, calls=%fused_computation.33 | convolution fusion | flops 3758096384 | bytes 15728640 | tf_op jit(solution)/shard_map/dot_general | solution.py:23
  76.7 6.8 %fusion.11 = f32[512,3584]{1,0:T(8,128)S(1)} fusion(bf16[512,1024]{1,0:T(8,128)(2,1)S(1)} %copy-done.3, bf16[1024,3584]{1,0:T(8,128)(2,1)} %param.8), kind=kOutput, calls=%fused_computation.34 | convolution fusion | flops 3758096384 | bytes 15728640 | tf_op jit(solution)/shard_map/dot_general | solution.py:24
  83.5 6.4 %pad_maximum_fusion = f32[512,7168]{1,0:T(8,128)} fusion(f32[512,3584]{1,0:T(8,128)S(1)} %fusion.11, f32[512,3584]{1,0:T(8,128)S(1)} %fusion.10), kind=kLoop, calls=%fused_computation | loop fusion | flops 3670016 | bytes 29360128 | tf_op jit(solution)/shard_map/concatenate | solution.py:21
  90.0 49.6 %reduce-scatter.9.cloned.1.call-done = f32[64,3584]{1,0:T(8,128)} async-done(((f32[512,3584]{1,0:T(8,128)}), f32[64,3584]{1,0:T(8,128)}) %reduce-scatter.9.cloned.1.call-update) | async-done | bytes 917520 | tf_op jit(solution)/shard_map/reduce_scatter | solution.py:51
  139.6 108.0 %reduce-scatter.5.cloned.1.call-done = f32[64,7168]{1,0:T(8,128)} async-done(((f32[512,7168]{1,0:T(8,128)}), f32[64,7168]{1,0:T(8,128)}) %reduce-scatter.5.cloned.1.call-update) | async-done | bytes 1835024 | tf_op jit(solution)/shard_map/reduce_scatter | solution.py:20
  250.8 8.8 %collective-permute-done = bf16[64,3584]{1,0:T(8,128)(2,1)S(1)} collective-permute-done((bf16[64,3584]{1,0:T(8,128)(2,1)S(1)}, bf16[64,3584]{1,0:T(8,128)(2,1)S(1)}, u32[]{:S(2)}, u32[]{:S(2)}) %collective-permute-start) | collective-permute-done | bytes 458784 | tf_op jit(solution)/shard_map/ppermute | solution.py:38
  259.6 12.1 %collective-permute-done.1 = bf16[64,3584]{1,0:T(8,128)(2,1)S(1)} collective-permute-done((bf16[64,3584]{1,0:T(8,128)(2,1)S(1)}, bf16[64,3584]{1,0:T(8,128)(2,1)S(1)}, u32[]{:S(2)}, u32[]{:S(2)}) %collective-permute-start.1) | collective-permute-done | bytes 458784 | tf_op jit(solution)/shard_map/ppermute | solution.py:38
  271.8 16.1 %collective-permute-done.2 = bf16[64,3584]{1,0:T(8,128)(2,1)S(1)} collective-permute-done((bf16[64,3584]{1,0:T(8,128)(2,1)S(1)}, bf16[64,3584]{1,0:T(8,128)(2,1)S(1)}, u32[]{:S(2)}, u32[]{:S(2)}) %collective-permute-start.2) | collective-permute-done | bytes 458784 | tf_op jit(solution)/shard_map/ppermute | solution.py:38
  287.8 8.8 %collective-permute-done.3 = bf16[64,3584]{1,0:T(8,128)(2,1)S(1)} collective-permute-done((bf16[64,3584]{1,0:T(8,128)(2,1)S(1)}, bf16[64,3584]{1,0:T(8,128)(2,1)S(1)}, u32[]{:S(2)}, u32[]{:S(2)}) %collective-permute-start.3) | collective-permute-done | bytes 458784 | tf_op jit(solution)/shard_map/ppermute | solution.py:38
  296.6 8.8 %collective-permute-done.4 = bf16[64,3584]{1,0:T(8,128)(2,1)S(1)} collective-permute-done((bf16[64,3584]{1,0:T(8,128)(2,1)S(1)}, bf16[64,3584]{1,0:T(8,128)(2,1)S(1)}, u32[]{:S(2)}, u32[]{:S(2)}) %collective-permute-start.4) | collective-permute-done | bytes 458784 | tf_op jit(solution)/shard_map/ppermute | solution.py:38
  305.4 8.8 %collective-permute-done.5 = bf16[64,3584]{1,0:T(8,128)(2,1)S(1)} collective-permute-done((bf16[64,3584]{1,0:T(8,128)(2,1)S(1)}, bf16[64,3584]{1,0:T(8,128)(2,1)S(1)}, u32[]{:S(2)}, u32[]{:S(2)}) %collective-permute-start.5) | collective-permute-done | bytes 458784 | tf_op jit(solution)/shard_map/ppermute | solution.py:38
  314.3 8.8 %collective-permute-done.6 = bf16[64,3584]{1,0:T(8,128)(2,1)} collective-permute-done((bf16[64,3584]{1,0:T(8,128)(2,1)S(1)}, bf16[64,3584]{1,0:T(8,128)(2,1)}, u32[]{:S(2)}, u32[]{:S(2)}) %collective-permute-start.6) | collective-permute-done | bytes 458784 | tf_op jit(solution)/shard_map/ppermute | solution.py:38
  328.9 7.3 %fusion.5 = bf16[512,1024]{1,0:T(8,128)(2,1)} fusion(bf16[3584,1024]{1,0:T(8,128)(2,1)} %param.9, bf16[1024,3584]{1,0:T(8,128)(2,1)S(1)} %constant_dynamic-update-slice_fusion, s32[]{:T(128)S(6)} %select_n.14), kind=kOutput, calls=%fused_computation.10 | convolution fusion | flops 3758620672 | bytes 12058628 | tf_op jit(solution)/shard_map/dot_general | solution.py:44
  336.5 7.4 %fusion.13 = f32[512,1024]{1,0:T(8,128)S(1)} fusion(bf16[512,3584]{1,0:T(8,128)(2,1)} %all-gather.9.cloned.1.call-done, bf16[1024,3584]{1,0:T(8,128)(2,1)} %param.7), kind=kOutput, calls=%fused_computation.36 | convolution fusion | flops 3758096384 | bytes 13107200 | tf_op jit(solution)/shard_map/dot_general | solution.py:8
  343.9 6.1 %all-gather.11.cloned.1.call-done = bf16[512,3584]{1,0:T(8,128)(2,1)} async-done(((bf16[64,3584]{1,0:T(8,128)(2,1)}), bf16[512,3584]{1,0:T(8,128)(2,1)}) %all-gather.11.cloned.1.call-update) | async-done | bytes 3670032 | tf_op jit(solution)/shard_map/all_gather | solution.py:58
  350.0 9.2 %add_convert_fusion = bf16[512,1024]{1,0:T(8,128)(2,1)} fusion(f32[512,1024]{1,0:T(8,128)S(1)} %fusion.13, bf16[512,3584]{1,0:T(8,128)(2,1)} %all-gather.11.cloned.1.call-done, bf16[1024,3584]{1,0:T(8,128)(2,1)} %param.8), kind=kOutput, calls=%fused_computation.9 | convolution fusion | flops 3759144960 | bytes 14155776 | tf_op jit(solution)/shard_map/dot_general | solution.py:8
  359.3 8.3 %convolution_convert_fusion = bf16[3584,1024]{1,0:T(8,128)(2,1)} fusion(bf16[512,1024]{1,0:T(8,128)(2,1)S(1)} %copy-done.2, bf16[1024,3584]{1,0:T(8,128)(2,1)} %copy-done, s32[]{:T(128)S(6)} %select_n.14), kind=kOutput, calls=%fused_computation.1 | convolution fusion | flops 3761766400 | bytes 12058628 | tf_op jit(solution)/shard_map/dot_general | solution.py:8
  373.7 10.0 %copy.10 = bf16[1024,3584]{1,0:T(8,128)(2,1)} copy(bf16[1024,3584]{0,1:T(8,128)(2,1)} %fusion) | data formatting | bytes 14680064
  383.6 8.2 %fusion.1 = bf16[1024,3584]{0,1:T(8,128)(2,1)} fusion(bf16[512,3584]{1,0:T(8,128)(2,1)} %all-gather.11.cloned.1.call-done, bf16[512,1024]{1,0:T(8,128)(2,1)S(1)} %copy-done.4), kind=kOutput, calls=%fused_computation.5 | convolution fusion | flops 3761766400 | bytes 12058624 | tf_op jit(solution)/shard_map/dot_general | solution.py:8
  391.8 10.0 %copy.11 = bf16[1024,3584]{1,0:T(8,128)(2,1)} copy(bf16[1024,3584]{0,1:T(8,128)(2,1)} %fusion.1) | data formatting | bytes 14680064
  401.8 7.1 %reduce-scatter.11.cloned.1.call-done = bf16[128,1024]{1,0:T(8,128)(2,1)} async-done(((bf16[512,1024]{1,0:T(8,128)(2,1)}), bf16[128,1024]{1,0:T(8,128)(2,1)}) %reduce-scatter.11.cloned.1.call-update) | async-done | bytes 262160 | tf_op jit(solution)/shard_map/reduce_scatter | solution.py:62
  (53 shorter events, 16.9 us)
Async XLA Ops:
  7.2 33.1 %all-gather.7.cloned.1.call-start = ((), (), s32[]{:S(2)}) async-start(), calls=%async_computation.7 | async-start | bytes 1310720 | tf_op jit(solution)/shard_map/all_gather | solution.py:16
  7.9 61.3 %all-gather.5.cloned.1.call-start = ((), (), s32[]{:S(2)}) async-start(), calls=%async_computation.4 | async-start | bytes 1310720 | tf_op jit(solution)/shard_map/all_gather | solution.py:15
  8.6 130.9 %reduce-scatter.9.cloned.1.call-start = ((), (), s32[]{:S(2)}) async-start(), calls=%async_computation.8 | async-start | bytes 8257536 | tf_op jit(solution)/shard_map/reduce_scatter | solution.py:51
  50.8 196.8 %reduce-scatter.5.cloned.1.call-start = ((), (), s32[]{:S(2)}) async-start(), calls=%async_computation.5 | async-start | bytes 16515072 | tf_op jit(solution)/shard_map/reduce_scatter | solution.py:20
  69.2 7.5 %copy-start.3 = (bf16[512,1024]{1,0:T(8,128)(2,1)S(1)}, bf16[512,1024]{1,0:T(8,128)(2,1)}, u32[]{:S(2)}) copy-start(bf16[512,1024]{1,0:T(8,128)(2,1)} %all-gather.5.cloned.1.call-done) | copy-start | bytes 3145732
  89.9 246.6 %all-gather.9.cloned.1.call-start = ((), (), s32[]{:S(2)}) async-start(), calls=%async_computation.9 | async-start | bytes 4128768 | tf_op jit(solution)/shard_map/all_gather | solution.py:57
  250.7 99.3 %all-gather.11.cloned.1.call-start = ((), (), s32[]{:S(2)}) async-start(), calls=%async_computation.10 | async-start | bytes 4128768 | tf_op jit(solution)/shard_map/all_gather | solution.py:58
  250.8 8.9 %collective-permute-start = (bf16[64,3584]{1,0:T(8,128)(2,1)S(1)}, bf16[64,3584]{1,0:T(8,128)(2,1)S(1)}, u32[]{:S(2)}, u32[]{:S(2)}) collective-permute-start(bf16[64,3584]{1,0:T(8,128)(2,1)S(1)} %get-tuple-element.12), channel_id=1, source_target_pairs={{0,4},{4,8},{8,12},{12,16},{16,20},{20,24},{24,28},{28,0},{1,5},{5... | collective-permute-start | bytes 1376264 | tf_op jit(solution)/shard_map/ppermute | solution.py:38
  259.6 12.1 %collective-permute-start.1 = (bf16[64,3584]{1,0:T(8,128)(2,1)S(1)}, bf16[64,3584]{1,0:T(8,128)(2,1)S(1)}, u32[]{:S(2)}, u32[]{:S(2)}) collective-permute-start(bf16[64,3584]{1,0:T(8,128)(2,1)S(1)} %collective-permute-done), channel_id=1, source_target_pairs={{0,4},{4,8},{8,12},{12,16},{16,20},{20,24},{24,28},{28,0},{1,5},{5... | collective-permute-start | bytes 1376264 | tf_op jit(solution)/shard_map/ppermute | solution.py:38
  271.8 16.1 %collective-permute-start.2 = (bf16[64,3584]{1,0:T(8,128)(2,1)S(1)}, bf16[64,3584]{1,0:T(8,128)(2,1)S(1)}, u32[]{:S(2)}, u32[]{:S(2)}) collective-permute-start(bf16[64,3584]{1,0:T(8,128)(2,1)S(1)} %collective-permute-done.1), channel_id=1, source_target_pairs={{0,4},{4,8},{8,12},{12,16},{16,20},{20,24},{24,28},{28,0},{1,5},{5... | collective-permute-start | bytes 1376264 | tf_op jit(solution)/shard_map/ppermute | solution.py:38
  287.8 8.8 %collective-permute-start.3 = (bf16[64,3584]{1,0:T(8,128)(2,1)S(1)}, bf16[64,3584]{1,0:T(8,128)(2,1)S(1)}, u32[]{:S(2)}, u32[]{:S(2)}) collective-permute-start(bf16[64,3584]{1,0:T(8,128)(2,1)S(1)} %collective-permute-done.2), channel_id=1, source_target_pairs={{0,4},{4,8},{8,12},{12,16},{16,20},{20,24},{24,28},{28,0},{1,5},{5... | collective-permute-start | bytes 1376264 | tf_op jit(solution)/shard_map/ppermute | solution.py:38
  296.6 8.8 %collective-permute-start.4 = (bf16[64,3584]{1,0:T(8,128)(2,1)S(1)}, bf16[64,3584]{1,0:T(8,128)(2,1)S(1)}, u32[]{:S(2)}, u32[]{:S(2)}) collective-permute-start(bf16[64,3584]{1,0:T(8,128)(2,1)S(1)} %collective-permute-done.3), channel_id=1, source_target_pairs={{0,4},{4,8},{8,12},{12,16},{16,20},{20,24},{24,28},{28,0},{1,5},{5... | collective-permute-start | bytes 1376264 | tf_op jit(solution)/shard_map/ppermute | solution.py:38
  305.4 8.8 %collective-permute-start.5 = (bf16[64,3584]{1,0:T(8,128)(2,1)S(1)}, bf16[64,3584]{1,0:T(8,128)(2,1)S(1)}, u32[]{:S(2)}, u32[]{:S(2)}) collective-permute-start(bf16[64,3584]{1,0:T(8,128)(2,1)S(1)} %collective-permute-done.4), channel_id=1, source_target_pairs={{0,4},{4,8},{8,12},{12,16},{16,20},{20,24},{24,28},{28,0},{1,5},{5... | collective-permute-start | bytes 1376264 | tf_op jit(solution)/shard_map/ppermute | solution.py:38
  314.2 8.9 %collective-permute-start.6 = (bf16[64,3584]{1,0:T(8,128)(2,1)S(1)}, bf16[64,3584]{1,0:T(8,128)(2,1)}, u32[]{:S(2)}, u32[]{:S(2)}) collective-permute-start(bf16[64,3584]{1,0:T(8,128)(2,1)S(1)} %collective-permute-done.5), channel_id=1, source_target_pairs={{0,4},{4,8},{8,12},{12,16},{16,20},{20,24},{24,28},{28,0},{1,5},{5... | collective-permute-start | bytes 1376264 | tf_op jit(solution)/shard_map/ppermute | solution.py:38
  314.3 87.5 %reduce-scatter.7.cloned.1.call-start = ((), (), s32[]{:S(2)}) async-start(), calls=%async_computation.6 | async-start | bytes 1310720 | tf_op jit(solution)/shard_map/reduce_scatter | solution.py:43
  325.8 3.1 copy-start
  336.3 72.6 %reduce-scatter.11.cloned.1.call-start = ((), (), s32[]{:S(2)}) async-start(), calls=%async_computation.11 | async-start | bytes 1310720 | tf_op jit(solution)/shard_map/reduce_scatter | solution.py:62
  343.9 15.4 %copy-start.2 = (bf16[512,1024]{1,0:T(8,128)(2,1)S(1)}, bf16[512,1024]{1,0:T(8,128)(2,1)}, u32[]{:S(2)}) copy-start(bf16[512,1024]{1,0:T(8,128)(2,1)} %all-gather.7.cloned.1.call-done) | copy-start | bytes 3145732
  359.3 8.3 %copy-start.1 = (bf16[512,3584]{1,0:T(8,128)(2,1)S(1)}, bf16[512,3584]{1,0:T(8,128)(2,1)}, u32[]{:S(2)}) copy-start(bf16[512,3584]{1,0:T(8,128)(2,1)} %all-gather.9.cloned.1.call-done) | copy-start | bytes 11010052
  359.3 8.3 %copy-start.4 = (bf16[512,1024]{1,0:T(8,128)(2,1)S(1)}, bf16[512,1024]{1,0:T(8,128)(2,1)}, u32[]{:S(2)}) copy-start(bf16[512,1024]{1,0:T(8,128)(2,1)} %all-gather.5.cloned.1.call-done) | copy-start | bytes 3145732
Sparse Core Ops, SparseCore 0:
  9.5 30.6 all-gather.6
  41.8 27.3 all-gather.4
  73.2 66.3 reduce-scatter.8
  142.9 104.5 reduce-scatter.4
  250.8 41.1 all-gather.8
  314.4 35.5 all-gather.10
  352.9 27.2 reduce-scatter.6
  383.1 25.7 reduce-scatter.10
